TPU v7x, 512 devices: a whole 4x8x8 slice. The times are simulated.
512 devices in a mesh: grp: 32 (over y, x), mem: 16 (over z, core).
Axes of the slice: x: 4, y: 8, z: 8, core: 2. Of those that a mesh axis runs over, the one named last changes fastest.
Arguments:
- a_tiles: bfloat16 [16384, 128, 128], P(('grp', 'mem')), may hold values from -0.5 to 0.5
- b_tiles: bfloat16 [128, 128, 128], P('grp'), may hold values from -6 to 6
- mask_ref: int32 [16384, 24], P(('grp', 'mem')), may hold values from 0 to 31, as said below
- b_ref: int32 [16384, 24], P(('grp', 'mem')), may hold values from 0 to 127
- tile_strip: int32 [16384], P(('grp', 'mem')), may hold values from 0 to 31
- item_count: int32 [512], P(('grp', 'mem')), may hold values from 8 to 32
Outputs:
- strip_count: float32 [1024], P(('grp', 'mem'))
Inputs may be any that keep to these rules, and one draw needn't show every extreme that they name: mask_ref[t, p] and t % 32 have the same remainder modulo the number of devices of axis mem.
All inputs are finite; a program needn't handle non-finite values.
Results may differ from a plain program's by a relative error of at most 0.0003.
Values may be sent and summed in bfloat16 or wider, within the bound.
A program may use at most 64 MiB of HBM per device.

v0:
```python
import jax
import jax.numpy as jnp
from jax import lax
from jax.sharding import Mesh
from jax.sharding import PartitionSpec as P

STRIP_DEV = 2
GRP = ("grp_0", "grp_1")
GRP_MEM = ("grp_0", "grp_1", "mem")


def gather_axes(x, axes, dim):
    result = x
    for number in range(len(axes) - 1, -1, -1):
        result = lax.all_gather(result, axes[number], axis=dim, tiled=True)
    return result


def cut_along(x, dim, peers):
    shape = x.shape
    tiles = x.reshape(*shape[:dim], peers, shape[dim] // peers, *shape[dim + 1 :])
    return jnp.moveaxis(tiles, dim, 0)


def sent_and_summed(x, axis, dim):
    peers = lax.axis_size(axis)
    tiles = lax.all_to_all(cut_along(x, dim, peers), axis, 0, 0, tiled=True)
    return jnp.sum(tiles, axis=0)


def tile_values(left, closers, refs, table, members):
    tiles = left.shape[0]
    side = left.shape[1]
    middles = table.shape[0]
    rounds = tiles // members
    wide = table.reshape(middles, side * side).astype(jnp.float32)
    grouped = left.reshape(rounds, members, side, side)
    pick = closers // members
    pick_hot = (pick[..., None] == jnp.arange(rounds, dtype=jnp.int32)).astype(jnp.float32)
    ref_hot = (refs[..., None] == jnp.arange(middles, dtype=jnp.int32)).astype(jnp.float32)
    weights = jnp.einsum("npk,npr->knr", pick_hot, ref_hot, precision=lax.Precision.HIGHEST)

    def one_closer(which):
        closing = lax.dynamic_index_in_dim(grouped, which, 0, keepdims=False)
        inner = jnp.einsum("rsij,sik->rsjk", grouped, closing, preferred_element_type=jnp.float32)
        return jnp.dot(inner.reshape(tiles, side * side), wide.T, precision=lax.Precision.HIGHEST)

    scores = lax.map(one_closer, jnp.arange(rounds, dtype=jnp.int32))
    return jnp.sum(weights * scores, axis=(0, 2))


def strip_table(values, strips, count):
    onehot = (strips[..., None] == jnp.arange(count, dtype=jnp.int32)).astype(jnp.float32)
    return jnp.einsum("...s,...->s", onehot, values, precision=lax.Precision.HIGHEST)


def shards(a_tiles, b_tiles, mask_ref, b_ref, tile_strip, item_count):
    members = lax.axis_size("mem")
    strip_group = STRIP_DEV * members
    tiles = a_tiles.shape[0]
    table = gather_axes(b_tiles, GRP, 0)
    live = (jnp.arange(tiles, dtype=jnp.int32) < item_count[0]).astype(jnp.float32)
    values = tile_values(a_tiles, mask_ref, b_ref, table, members) * live
    sums = strip_table(values, tile_strip, strip_group)
    return sent_and_summed(sums, "mem", 0)


def solution(mesh):
    split = Mesh(mesh.devices.reshape(8, 4, mesh.shape["mem"]), ("grp_0", "grp_1", "mem"))
    in_specs = (
        P(GRP_MEM, None, None),
        P(GRP, None, None),
        P(GRP_MEM, None),
        P(GRP_MEM, None),
        P(GRP_MEM),
        P(GRP_MEM),
    )
    out_specs = P(GRP_MEM)
    return jax.shard_map(
        shards, mesh=split, in_specs=in_specs, out_specs=out_specs, check_vma=False
    )
```

profile of v0, /device:TPU:1, one launch (start us, length us, event | category | flops | bytes accessed | tf_op | source)
XLA Modules:
  0.0 149.6 jit_solution(7007980717978741917)
XLA Ops:
  6.5 0.0 copy-start.1
  6.5 0.0 copy-start
  6.5 0.0 all-gather.2.cloned.1.call-start
  6.5 13.4 %all_gather.6 = bf16[16,128,128]{2,1,0:T(8,128)(2,1)} all-gather(bf16[4,128,128]{2,1,0:T(8,128)(2,1)} %param.9), channel_id=1, replica_groups=mesh['grp_0'=8,'grp_1'=4,'mem'=16] {'grp_1'}, dimensions={0}, use_global_device_ids=true | all-gather | bytes 655360 | tf_op jit(solution)/shard_map/all_gather | solution.py:15
  20.0 0.0 all-gather.2.cloned.1.call-update
  20.0 1.3 copy.19
  21.3 0.0 copy-done.1
  21.3 0.1 copy.18
  21.4 0.0 copy-done
  21.4 0.1 copy.17
  22.1 60.6 %all-gather.2.cloned.1.call-done = bf16[128,128,128]{2,1,0:T(8,128)(2,1)} async-done(((bf16[16,128,128]{2,1,0:T(8,128)(2,1)}), bf16[128,128,128]{2,1,0:T(8,128)(2,1)}) %all-gather.2.cloned.1.call-update) | async-done | bytes 4194320 | tf_op jit(solution)/shard_map/all_gather | solution.py:15
  82.7 8.8 %copy.34 = f32[16,8,128,128]{3,1,2,0:T(8,128)} copy(bf16[16,8,128,128]{3,2,1,0:T(8,128)(2,1)} %bitcast.58) | data formatting | bytes 12582912
  91.5 0.0 copy-start.2
  91.5 34.8 %while.10 = (s32[]{:T(128)}, f32[2,32,128]{2,0,1:T(2,128)S(1)}, s32[2]{0:T(128)S(1)}, bf16[2,16,128,128]{3,2,0,1:T(8,128)(2,1)S(1)}, f32[128,16384]{1,0:T(8,128)}, /*index=5*/s32[]{:T(128)}, s32[]{:T(128)}, s32[]{:T(128)}) while((s32[]{:T(128)}, f32[2,32,128]{2,0,1:T(2,128)S(1)}, s32[2]{0:T(128)S(1)}, bf16[2,16,128,128]{3,2,0,1:T(8,128)(2,1)S(1)}, ...), condition=%wide.region_1.2_spmd, body=%wide.region_0.1_spmd.sunk | while | flops 939524096 | bytes 18399372 | solution.py:48
  91.5 0.6 dynamic_slice.15
  93.8 1.9 %convolution_bitcast_fusion.4 = f32[2,16,128,128]{2,3,0,1:T(8,128)} fusion(bf16[2,16,128,128]{3,2,0,1:T(8,128)(2,1)S(1)} %get-tuple-element.103, s32[]{:T(128)S(6)} %select_n.12), kind=kOutput, calls=%fused_computation.3.clone.1 | convolution fusion | flops 134217728 | bytes 3670020 | tf_op jit(solution)/shard_map/while/body/eval_jaxpr/rsij,sik->rsjk/dot_general | solution.py:45
  95.7 1.9 %copy.38 = f32[2,16,128,128]{3,2,1,0:T(8,128)S(1)} copy(f32[2,16,128,128]{2,3,0,1:T(8,128)} %convolution_bitcast_fusion.4) | data formatting | bytes 4194304 | tf_op jit(solution)/shard_map/while/body/eval_jaxpr/rsij,sik->rsjk/transpose | solution.py:45
  97.6 11.2 %fusion.32 = f32[32,128]{1,0:T(8,128)S(1)} fusion(f32[128,16384]{1,0:T(8,128)} %get-tuple-element.104, f32[4,8,128,128]{3,2,1,0:T(8,128)S(1)} %bitcast.57), kind=kOutput, calls=%fused_computation.clone.1 | convolution fusion | flops 805306368 | bytes 10502144 | tf_op jit(solution)/shard_map/while/body/eval_jaxpr/dot_general | solution.py:46
  108.8 0.1 dynamic_update_slice.5
  108.9 0.6 dynamic_slice.15
  111.3 1.9 %convolution_bitcast_fusion.4 = f32[2,16,128,128]{2,3,0,1:T(8,128)} fusion(bf16[2,16,128,128]{3,2,0,1:T(8,128)(2,1)S(1)} %get-tuple-element.103, s32[]{:T(128)S(6)} %select_n.12), kind=kOutput, calls=%fused_computation.3.clone.1 | convolution fusion | flops 134217728 | bytes 3670020 | tf_op jit(solution)/shard_map/while/body/eval_jaxpr/rsij,sik->rsjk/dot_general | solution.py:45
  113.1 1.9 %copy.38 = f32[2,16,128,128]{3,2,1,0:T(8,128)S(1)} copy(f32[2,16,128,128]{2,3,0,1:T(8,128)} %convolution_bitcast_fusion.4) | data formatting | bytes 4194304 | tf_op jit(solution)/shard_map/while/body/eval_jaxpr/rsij,sik->rsjk/transpose | solution.py:45
  115.1 11.2 %fusion.32 = f32[32,128]{1,0:T(8,128)S(1)} fusion(f32[128,16384]{1,0:T(8,128)} %get-tuple-element.104, f32[4,8,128,128]{3,2,1,0:T(8,128)S(1)} %bitcast.57), kind=kOutput, calls=%fused_computation.clone.1 | convolution fusion | flops 805306368 | bytes 10502144 | tf_op jit(solution)/shard_map/while/body/eval_jaxpr/dot_general | solution.py:46
  126.3 0.1 dynamic_update_slice.5
  126.4 0.5 fusion.7
  126.9 0.0 copy-done.2
  126.9 0.2 convolution_bitcast_fusion.2
  127.1 0.1 all_to_all.6
  127.2 15.1 %all_to_all.9 = f32[16,1,2]{2,1,0:T(1,128)S(1)} all-to-all(f32[16,1,2]{2,1,0:T(1,128)S(1)} %bitcast.61), channel_id=1, replica_groups=mesh['grp_0'=8,'grp_1'=4,'mem'=16] {'mem'}, dimensions={0} | all-to-all | bytes 256 | tf_op jit(solution)/shard_map/all_to_all | solution.py:27
  142.2 0.5 reduce_sum.19
  (3 shorter events, 0.0 us)
Async XLA Ops:
  6.5 14.8 %copy-start.1 = (s32[32,24]{0,1:T(8,128)S(1)}, s32[32,24]{0,1:T(8,128)}, u32[]{:S(2)}) copy-start(s32[32,24]{0,1:T(8,128)} %param.10) | copy-start | bytes 9220
  6.5 14.9 %copy-start = (s32[32,24]{0,1:T(8,128)S(1)}, s32[32,24]{0,1:T(8,128)}, u32[]{:S(2)}) copy-start(s32[32,24]{0,1:T(8,128)} %param.11) | copy-start | bytes 9220
  6.5 76.1 %all-gather.2.cloned.1.call-start = ((), (), s32[]{:S(2)}) async-start(), calls=%async_computation.1 | async-start | bytes 4718592 | tf_op jit(solution)/shard_map/all_gather | solution.py:15
  91.5 35.4 %copy-start.2 = (s32[32]{0:T(128)S(1)}, s32[32]{0:T(128)}, u32[]{:S(2)}) copy-start(s32[32]{0:T(128)} %param.12) | copy-start | bytes 388
Sparse Core Ops, SparseCore 0:
  20.1 62.5 all-gather.1
where the time goes:
time: 150 us
  waiting for transfers between devices  60.6 us (40%)
  blocking collectives  28.5 us (19%)
  matrix products  26.8 us (18%)
  local copies, waits for them, and re-layouts  15.6 us (10%)
  between operations  14.1 us (9%)
  loops' own time  3.51 us (2%)
    all_gather x1, waiting for transfers between devices, gather_axes(): result = lax.all_gather(result, axes[number], axis=dim, tiled=True)  60.6 us
    dot_general x2, matrix products, one_closer(): jnp.dot(inner.reshape(tiles, side * side), wide.T, precision=lax.Precisio...  22.4 us
    all_to_all x1, blocking collectives, sent_and_summed(): tiles = lax.all_to_all(cut_along(x, dim, peers), axis, 0, 0, tiled=True)  15.1 us
    all_gather x1, blocking collectives, gather_axes(): result = lax.all_gather(result, axes[number], axis=dim, tiled=True)  13.4 us
    unnamed x8, local copies, waits for them, and re-layouts  8.92 us
    transpose x2, local copies, waits for them, and re-layouts, one_closer(): jnp.einsum('rsij,sik->rsjk', grouped, closing, preferred_element_type=jnp...  3.86 us
    dot_general x2, matrix products, one_closer(): jnp.einsum('rsij,sik->rsjk', grouped, closing, preferred_element_type=jnp...  3.74 us
    another operation x1, loops' own time, tile_values(): scores = lax.map(one_closer, jnp.arange(rounds, dtype=jnp.int32))  3.51 us
  transfers between devices with their start and end apart: 1, of which 1 were waited for; matrix products, arithmetic and copies ran while one was open for 1% of the time, Pallas kernels for 0%

commit v1 on v0

v1 whole, which is shorter than its diff:
```python
import jax
import jax.numpy as jnp
from jax import lax
from jax.experimental import pallas as pl
from jax.experimental.pallas import tpu as pltpu
from jax.sharding import PartitionSpec as P

NX, NY, NZ = 4, 8, 8
TILE = 128
ITEM_DEV = 32
PARTNERS = 24
HOPS = (0, 1, 7, 2, 6, 3, 5, 4)
MESH = pl.DeviceIdType.MESH
F32, BF16, I32 = jnp.float32, jnp.bfloat16, jnp.int32


def iota(shape, dim):
    return lax.broadcasted_iota(I32, shape, dim)


def kernel(a_hbm, b_hbm, mask_ref, bref_ref, strip_ref, count_ref, out_ref,
           a_buf, m_buf, n_buf, meta, g_buf, kw_buf, oh_buf, acc, p_buf, r_buf,
           loc_sem, y_s, y_r, x_s, x_r, f_s, f_r, z_s, z_r, c_s, c_r, e_s, e_r):
    grp = lax.axis_index("grp")
    mem = lax.axis_index("mem")
    gy, gx = grp // NX, grp % NX
    z, core = mem // 2, mem % 2
    u = z % 2
    zu = ((z + 1) % NZ) * 2 + core
    zd = ((z + NZ - 1) % NZ) * 2 + core
    xr = gy * NX + (gx + 1) % NX
    xl = gy * NX + (gx + NX - 1) % NX
    ydev = [((gy + HOPS[q]) % NY) * NX + gx for q in range(NY)]
    sib = z * 2 + (1 - core)

    own_m = pltpu.make_async_copy(b_hbm.at[2 * core + u], m_buf.at[0], loc_sem.at[0])
    own_n = pltpu.make_async_copy(b_hbm.at[2 * core + (1 - u)], n_buf.at[0], loc_sem.at[1])
    own_a = pltpu.make_async_copy(a_hbm, a_buf.at[pl.ds(0, ITEM_DEV)], loc_sem.at[2])
    own_m.start()
    own_a.start()
    own_n.start()

    barrier = pltpu.get_barrier_semaphore()
    for q in range(1, NY):
        pl.semaphore_signal(barrier, inc=1, device_id=(ydev[q], mem), device_id_type=MESH)
    for gg in (xl, xr):
        pl.semaphore_signal(barrier, inc=1, device_id=(gg, mem), device_id_type=MESH)
    for o in range(1, 16):
        pl.semaphore_signal(barrier, inc=1, device_id=(grp, (mem + o) % 16), device_id_type=MESH)

    meta[0] = jnp.full((32, 128), -1, I32)
    meta[0, 0:PARTNERS, 0:ITEM_DEV] = bref_ref[...] + 128 * (mask_ref[...] >> 4)
    lane = iota((1, ITEM_DEV), 1)
    meta[0, PARTNERS:PARTNERS + 1, 0:ITEM_DEV] = jnp.where(lane < count_ref[0], strip_ref[...], -1)
    acc[...] = jnp.zeros(acc.shape, F32)

    own_m.wait()
    pl.semaphore_wait(barrier, 24)

    def remote(src, dst, ss, rs, dev):
        return pltpu.make_async_remote_copy(
            src_ref=src, dst_ref=dst, send_sem=ss, recv_sem=rs, device_id=dev, device_id_type=MESH)

    def slot(q, dx):
        return q * 4 + dx

    ycopy = [None] + [
        remote(m_buf.at[0], m_buf.at[slot(q, 0)], y_s.at[q], y_r.at[q], (ydev[q], mem)) for q in range(1, NY)]
    xright = [remote(m_buf.at[slot(q, 0)], m_buf.at[slot(q, 1)], x_s.at[q], x_r.at[q], (xr, mem)) for q in range(NY)]
    xleft = [remote(m_buf.at[slot(q, 0)], m_buf.at[slot(q, 3)], x_s.at[8 + q], x_r.at[8 + q], (xl, mem)) for q in range(NY)]
    fwd = [remote(m_buf.at[slot(q, 1 if q % 2 == 0 else 3)], m_buf.at[slot(q, 2)], f_s.at[q], f_r.at[q],
                  (xr if q % 2 == 0 else xl, mem)) for q in range(NY)]
    zcopy = [None] + [
        remote(m_buf.at[s], n_buf.at[s], z_s.at[s], z_r.at[s], (grp, zu if (s // 4 + s) % 2 == 0 else zd))
        for s in range(1, 32)]
    metacopy = remote(meta.at[0], meta.at[1], c_s.at[0], c_r.at[0], (grp, sib))
    acopy = remote(a_buf.at[pl.ds(0, ITEM_DEV)], a_buf.at[pl.ds(ITEM_DEV, ITEM_DEV)], c_s.at[1], c_r.at[1], (grp, sib))

    xright[0].start()
    xleft[0].start()
    for q in range(1, NY):
        ycopy[q].start()
    metacopy.start()
    own_a.wait()
    acopy.start()

    def products(d):
        def body(i, carry):
            x = jnp.concatenate([a_buf[d * 32 + i], a_buf[d * 32 + 16 + i]], axis=1)
            c = lax.dot_general(x, x, (((0,), (0,)), ((), ())), preferred_element_type=F32)
            for ti in range(2):
                for k in range(2):
                    g_buf[k * 64 + d * 32 + ti * 16 + i] = c[ti * 128:(ti + 1) * 128, k * 128:(k + 1) * 128]
            return carry
        return body

    def got_y(q):
        ycopy[q].wait_recv()
        xright[q].start()
        xleft[q].start()
        zcopy[slot(q, 0)].start()

    def got_x(q):
        xright[q].wait_recv()
        xleft[q].wait_recv()
        fwd[q].start()
        zcopy[slot(q, 1)].start()
        zcopy[slot(q, 3)].start()

    def got_f(q):
        fwd[q].wait_recv()
        zcopy[slot(q, 2)].start()

    def build_weights():
        metacopy.wait_recv()
        codes = jnp.concatenate([meta[0, 0:PARTNERS, 0:32], meta[1, 0:PARTNERS, 0:32]], axis=1)
        r = iota((64, 1), 0)
        s = r % 32
        q, dx = s // 4, s % 4
        hop = jnp.zeros((64, 1), I32)
        for n in range(1, NY):
            hop = jnp.where(q == n, HOPS[n], hop)
        owner = ((gy + NY - hop) % NY) * NX + (gx + NX - dx) % NX
        tile = owner * 4 + 2 * core + jnp.where(r < 32, u, 1 - u)
        parts = []
        for k in range(2):
            w = jnp.zeros((64, 64), F32)
            for p in range(PARTNERS):
                w = w + (codes[p:p + 1, :] == tile + 128 * k).astype(F32)
            parts.append(w)
        w = jnp.concatenate(parts, axis=1).astype(BF16)
        spread = (iota((64, 1024), 0) == iota((64, 1024), 1) // 16).astype(BF16)
        wide = lax.dot_general(w, spread, (((0,), (0,)), ((), ())), preferred_element_type=F32)
        diag = (iota((256, 1024), 0) % 16 == iota((256, 1024), 1) % 16).astype(F32)
        for nb in range(8):
            rows = jnp.broadcast_to(wide[nb * 16:(nb + 1) * 16, None, :], (16, 16, 1024)).reshape(256, 1024)
            kw_buf[nb] = (rows * diag).astype(BF16)
        row = iota((128, 128), 0)
        target = jnp.where(row % 8 < 2, (row // 8) * 2 + row % 8, -2)
        oh = jnp.zeros((128, 1024), F32)
        for d in range(2):
            hot = (target == meta[d, PARTNERS:PARTNERS + 1, :]).astype(BF16)
            rep = ((iota((128, 1024), 1) // 8) % 64 - d * 32 == iota((128, 1024), 0)).astype(BF16)
            oh = oh + jnp.dot(hot, rep, preferred_element_type=F32)
        oh_buf[...] = oh.astype(BF16)

    def run_pass(buf, s0, rb):
        def body(nb, carry):
            lhs = kw_buf[nb, :, rb * 256:(rb + 1) * 256]
            n0 = pl.multiple_of(nb * 16, 16)
            total = acc[pl.ds(n0, 16)]
            for jp in range(4):
                j = jp * 32
                right = jnp.concatenate([buf[s0:s0 + 16, j:j + 16, :].reshape(256, 128),
                                         buf[s0:s0 + 16, j + 16:j + 32, :].reshape(256, 128)], axis=1)
                w = jnp.dot(lhs, right, preferred_element_type=F32)
                g0 = g_buf[pl.ds(n0, 16), j:j + 16, :]
                g1 = g_buf[pl.ds(n0, 16), j + 16:j + 32, :]
                prod = w[:, :128].reshape(16, 16, 128) * g0 + w[:, 128:].reshape(16, 16, 128) * g1
                total = total + (prod[:, :8] + prod[:, 8:])
            acc[pl.ds(n0, 16)] = total
            return carry
        lax.fori_loop(0, 8, body, 0)

    lax.fori_loop(0, 8, products(0), 0)
    got_x(0)
    got_y(1)
    got_y(2)
    lax.fori_loop(8, 16, products(0), 0)
    got_f(0)
    got_x(1)
    got_x(2)
    got_y(3)
    got_y(4)
    build_weights()
    got_f(1)
    got_f(2)
    got_x(3)
    got_x(4)
    got_y(5)
    got_y(6)
    acopy.wait_recv()
    lax.fori_loop(0, 8, products(1), 0)
    got_f(3)
    got_f(4)
    got_x(5)
    got_x(6)
    got_y(7)
    lax.fori_loop(8, 16, products(1), 0)
    got_f(5)
    got_f(6)
    got_x(7)
    run_pass(m_buf, 0, 0)
    got_f(7)
    run_pass(m_buf, 16, 1)
    own_n.wait()
    for s in range(1, 16):
        zcopy[s].wait_recv()
    run_pass(n_buf, 0, 2)
    for s in range(16, 32):
        zcopy[s].wait_recv()
    run_pass(n_buf, 16, 3)

    rest = acc[...].reshape(1024, 128)
    sums = jnp.zeros((128, 128), F32)
    for _ in range(3):
        part = rest.astype(BF16)
        rest = rest - part.astype(F32)
        sums = sums + jnp.dot(oh_buf[...], part, preferred_element_type=F32)
    p_buf[...] = sums.reshape(16, 8, 128)

    ends = [None] + [
        remote(p_buf.at[(mem + o) % 16], r_buf.at[o], e_s.at[o], e_r.at[o], (grp, (mem + o) % 16))
        for o in range(1, 16)]
    for o in range(1, 16):
        ends[o].start()
    total = p_buf[mem]
    for o in range(1, 16):
        ends[o].wait_recv()
        total = total + r_buf[o]
    out_ref[0] = jnp.sum(total[0:1, :])
    out_ref[1] = jnp.sum(total[1:2, :])

    for copy in ycopy[1:] + xright + xleft + fwd + zcopy[1:] + [metacopy, acopy] + ends[1:]:
        copy.wait_send()


def shards(a_tiles, b_tiles, mask_ref, b_ref, tile_strip, item_count):
    dma = pltpu.SemaphoreType.DMA
    return pl.pallas_call(
        kernel,
        out_shape=jax.ShapeDtypeStruct((2,), F32),
        in_specs=[
            pl.BlockSpec(memory_space=pl.ANY),
            pl.BlockSpec(memory_space=pl.ANY),
            pl.BlockSpec(memory_space=pltpu.VMEM),
            pl.BlockSpec(memory_space=pltpu.VMEM),
            pl.BlockSpec(memory_space=pltpu.VMEM),
            pl.BlockSpec(memory_space=pltpu.SMEM),
        ],
        out_specs=pl.BlockSpec(memory_space=pltpu.SMEM),
        scratch_shapes=[
            pltpu.VMEM((64, TILE, TILE), BF16),
            pltpu.VMEM((32, TILE, TILE), BF16),
            pltpu.VMEM((32, TILE, TILE), BF16),
            pltpu.VMEM((2, 32, 128), I32),
            pltpu.VMEM((128, TILE, TILE), F32),
            pltpu.VMEM((8, 256, 1024), BF16),
            pltpu.VMEM((128, 1024), BF16),
            pltpu.VMEM((128, 8, 128), F32),
            pltpu.VMEM((16, 8, 128), F32),
            pltpu.VMEM((16, 8, 128), F32),
            dma((3,)),
            dma((8,)), dma((8,)),
            dma((16,)), dma((16,)),
            dma((8,)), dma((8,)),
            dma((32,)), dma((32,)),
            dma((2,)), dma((2,)),
            dma((16,)), dma((16,)),
        ],
        compiler_params=pltpu.CompilerParams(
            collective_id=0, has_side_effects=True, vmem_limit_bytes=56 * 1024 * 1024),
    )(a_tiles, b_tiles, mask_ref.T, b_ref.T, tile_strip.reshape(1, ITEM_DEV), item_count)


def solution(mesh):
    both = ("grp", "mem")
    in_specs = (P(both, None, None), P("grp", None, None), P(both, None), P(both, None), P(both), P(both))
    return jax.shard_map(shards, mesh=mesh, in_specs=in_specs, out_specs=P(both), check_vma=False)
```

time: 150 us -> 55.5 us (0.37)
  waiting for transfers between devices: 60.6 us -> 0 us
  Pallas kernels: 0 us -> 53.4 us
  blocking collectives: 28.5 us -> 0 us
  matrix products: 26.8 us -> 0 us
  local copies, waits for them, and re-layouts: 15.6 us -> 1.19 us
  between operations: 14.1 us -> 0.66 us
  loops' own time: 3.51 us -> 0 us
    all_gather x1 -> x0, waiting for transfers between devices: 60.6 us -> none  [gather_axes(): result = lax.all_gather(result, axes[number], axis=dim, tiled=True)]
    pallas_call x0 -> x1, Pallas kernels: none -> 53.4 us  [shards(): pl.pallas_call(kernel, out_shape=jax.ShapeDtypeStruct((2,), F32), in_spec...]
    dot_general x6 -> x0, matrix products: 26.8 us -> none  [the longest x2 22.4 us: one_closer(): jnp.dot(inner.reshape(tiles, side * side), wide.T, precision=lax.Precisio...]
    all_to_all x1 -> x0, blocking collectives: 15.1 us -> none  [sent_and_summed(): tiles = lax.all_to_all(cut_along(x, dim, peers), axis, 0, 0, tiled=True)]
    all_gather x1 -> x0, blocking collectives: 13.4 us -> none  [gather_axes(): result = lax.all_gather(result, axes[number], axis=dim, tiled=True)]
    unnamed x8 -> x1, local copies, waits for them, and re-layouts: 8.92 us -> 1.19 us
    transpose x2 -> x0, local copies, waits for them, and re-layouts: 3.86 us -> none  [one_closer(): jnp.einsum('rsij,sik->rsjk', grouped, closing, preferred_element_type=jnp...]
    another operation x1 -> x0, loops' own time: 3.51 us -> none  [tile_values(): scores = lax.map(one_closer, jnp.arange(rounds, dtype=jnp.int32))]
  transfers between devices with their start and end apart: 1 -> 0, of which waited for: 1 -> 0; matrix products, arithmetic and copies ran while one was open for 1% -> 0% of each run, Pallas kernels for 0% -> 0%
where the time goes in v1:
time: 55.5 us; the launch traced here: 55.3 us
  Pallas kernels  53.4 us (96%)
  local copies, waits for them, and re-layouts  1.19 us (2%)
  between operations  0.66 us (1%)
    pallas_call x1, Pallas kernels, shards(): pl.pallas_call(kernel, out_shape=jax.ShapeDtypeStruct((2,), F32), in_spec...  53.4 us
    unnamed x1, local copies, waits for them, and re-layouts  1.19 us

profile of v1, /device:TPU:1, one launch (start us, length us, event | category | flops | bytes accessed | tf_op | source)
XLA Modules:
  0.0 55.3 jit_solution(9545633999201211928)
XLA Ops:
  0.7 53.4 %shard_map.64 = f32[2]{0:T(128)} custom-call(bf16[32,128,128]{2,1,0:T(8,128)(2,1)} %a_hbm.1, bf16[4,128,128]{2,1,0:T(8,128)(2,1)} %b_hbm.1, s32[24,32]{1,0:T(8,128)} %bitcast.3, s32[24,32]{1,0:T(8,128)} %bitcast.4, s32[1,32]{1,0:T(1,128)} %bitcast.5, s32[1]{0:T(128)S(6)} %copy.8.count_ref), custom_call_target="tpu_custom_call" | custom-call | tf_op jit(solution)/shard_map/pallas_call | solution.py:230
  54.1 1.2 %copy.9 = f32[2]{0:T(128)} copy(f32[2]{0:T(128)} %shard_map.64) | data formatting | bytes 16
